TPU v7x, 256 devices: a whole 4x4x8 slice. The times are simulated.
256 devices in a mesh: blk: 64 (over y_hi, x, z), grp: 4 (over y_lo, core).
Axes of the slice: x: 4, y: 4 (y_hi: 2, y_lo: 2; y = y_hi * 2 + y_lo), z: 8, core: 2. Of those that a mesh axis runs over, the one named last changes fastest.
Arguments:
- queries: float32 [32768, 256], P(('blk', 'grp')), may hold values from -20 to 20
- queue: float32 [131072, 256], P(('blk', 'grp')), may hold values from -16 to 16
- new_keys: float32 [32768, 256], P(('blk', 'grp')), may hold values from -3.6 to 3.6
- pos_index: int32 [32768], P(('blk', 'grp')), may hold values from 0 to 32767, as said below
- pointer: int32 [1], replicated, may hold values from 0 to 3
Outputs:
- losses: float32 [32768], P(('blk', 'grp'))
- queue_next: float32 [131072, 256], P(('blk', 'grp'))
Inputs may be any that keep to these rules, and one draw needn't show every extreme that they name: pos_index of a query lies in the same aligned block of 128 rows as the query itself, and within each block every row is named exactly once.
All inputs are finite; a program needn't handle non-finite values.
Results may differ from a plain program's by a relative error of at most 0.0012.
Values may be sent and summed in bfloat16 or wider, within the bound.
No kernel may reach another device: no remote copies, remote signals or barrier semaphores. Data moves between devices by JAX's collectives and lax.ppermute only.
A program may use at most 64 MiB of HBM per device.

v0:
```python
import jax
import jax.numpy as jnp
from jax import lax
from jax.sharding import Mesh
from jax.sharding import PartitionSpec as P

BLK = ("blk_0", "blk_1", "blk_2")
BLK_GRP = ("blk_0", "blk_1", "blk_2", "grp")
logit_scale = 5.0
epsilon = 1e-06


def in_order(pieces, dim):
    dims = list(pieces.shape[1:])
    dims[dim] *= pieces.shape[0]
    return jnp.moveaxis(pieces, 0, dim).reshape(dims)


def gather_in_order(x, axes, sequence):
    pieces = x[None]
    for k in sequence:
        pieces = lax.all_gather(pieces, axes[k], axis=0, tiled=True)
    block = [lax.axis_size(axes[k]) for k in reversed(sequence)]
    pieces = pieces.reshape(*block, *x.shape)
    turned = sorted(range(len(sequence)), key=lambda place: sequence[len(sequence) - 1 - place])
    return pieces.transpose(*turned, *range(len(sequence), pieces.ndim)).reshape(-1, *x.shape)


def gather_axes(x, axes, sequence, dim):
    return in_order(gather_in_order(x, axes, sequence), dim)


def from_everyone(x, axis):
    count = lax.axis_size(axis)
    return lax.all_to_all(jnp.broadcast_to(x[None], (count, *x.shape)), axis, 0, 0, tiled=True)


def gather_directly(x, axis, dim):
    pieces = from_everyone(x, axis)
    return in_order(pieces, dim)


def collected_together(x, axis):
    leaves = jax.tree.leaves(x)
    sequence = sorted(range(len(leaves)), key=lambda k: -leaves[k].size)
    width = (1, *leaves[sequence[0]].shape)[-1]
    lines = [
        jnp.pad(leaves[k].reshape(-1), (0, -leaves[k].size % width)).reshape(-1, width)
        for k in sequence
    ]
    both, at, found = (lax.all_gather(jnp.concatenate(lines), axis), 0, {})
    for k, line in zip(sequence, lines):
        share = both[:, at : at + len(line)].reshape(len(both), -1)
        found[k] = share[:, : leaves[k].size].reshape(-1, *leaves[k].shape)
        at += len(line)
    numbers = iter(range(len(leaves)))
    return jax.tree.map(lambda _: found[next(numbers)], x)


def combined_by_axis(x, axes, combine):
    for axis in axes:
        pieces = collected_together(x, axis)
        x = jax.tree.map(lambda part: part[0], pieces)
        for k in range(1, lax.axis_size(axis)):
            x = combine(x, jax.tree.map(lambda part: part[k], pieces))
    return x


def from_behind(value, axis, steps):
    count = lax.axis_size(axis)
    pairs = [(source, (source + steps) % count) for source in range(count)]
    return lax.ppermute(value, axis, pairs)


def normalize(rows):
    return rows / jnp.sqrt(jnp.sum(rows * rows, axis=1, keepdims=True) + epsilon)


def block_size(count, limit):
    size_now = max(1, min(count, limit))
    while count % size_now != 0:
        size_now = size_now - 1
    return size_now


def make_fold(query_rows, carry, piece):
    count = piece.shape[0]
    step_rows = block_size(count, max(8, 2**21 // query_rows.shape[0]))
    blocks = piece.reshape(count // step_rows, step_rows, piece.shape[1])

    def one_block(state, key_block):
        top, total = state
        scores = logit_scale * lax.dot_general(
            query_rows, key_block, (((1,), (1,)), ((), ())), preferred_element_type=jnp.float32
        )
        new_top = jnp.maximum(top, jnp.max(scores, axis=1))
        total = total * jnp.exp(top - new_top) + jnp.sum(jnp.exp(scores - new_top[:, None]), axis=1)
        return ((new_top, total), None)

    result, unused = lax.scan(one_block, carry, blocks)
    return result


def combine(first, second):
    new_top = jnp.maximum(first[0], second[0])
    total = first[1] * jnp.exp(first[0] - new_top) + second[1] * jnp.exp(second[0] - new_top)
    return (new_top, total)


def finish(query_rows, top, total, positive_rows):
    pos = logit_scale * jnp.sum(
        query_rows.astype(jnp.float32) * positive_rows.astype(jnp.float32), axis=1
    )
    high = jnp.maximum(top, pos)
    return high + jnp.log(jnp.exp(pos - high) + total * jnp.exp(top - high)) - pos


def per_device(queries, queue, new_keys, pos_index, pointer):
    qhat = normalize(queries).astype(jnp.bfloat16)
    keys = queue.astype(jnp.bfloat16)
    count = qhat.shape[0]
    device_rank = lax.axis_index(BLK) * lax.axis_size("grp") + lax.axis_index("grp")
    base = device_rank * count
    positives = jnp.take(new_keys.astype(jnp.bfloat16), pos_index - base, axis=0)
    group = gather_axes(qhat, BLK, (0, 1, 2), 0)
    rows_all = group.shape[0]
    start_state = (jnp.full((rows_all,), -1e30, jnp.float32), jnp.zeros((rows_all,), jnp.float32))
    partial_value = make_fold(group, start_state, gather_directly(keys, "grp", 0))
    top_all, total_all = combined_by_axis(partial_value, BLK, combine)
    offset = lax.axis_index(BLK) * count
    top = lax.dynamic_slice_in_dim(top_all, offset, count, 0)
    total = lax.dynamic_slice_in_dim(total_all, offset, count, 0)
    losses = finish(qhat, top, total, positives)
    incoming = from_behind(new_keys, BLK_GRP, 1)
    start = pointer[0] * new_keys.shape[0]
    queue_next = lax.dynamic_update_slice(queue, incoming, (start, jnp.int32(0)))
    return (losses, queue_next)


def solution(mesh):
    finer = Mesh(
        mesh.devices.reshape(2, 4, 8, mesh.shape["grp"]), ("blk_0", "blk_1", "blk_2", "grp")
    )
    return jax.shard_map(
        per_device,
        mesh=finer,
        in_specs=(P(BLK_GRP, None), P(BLK_GRP, None), P(BLK_GRP, None), P(BLK_GRP), P()),
        out_specs=(P(BLK_GRP), P(BLK_GRP, None)),
        check_vma=False,
    )
```

profile of v0, /device:TPU:8, one launch (start us, length us, event | category | flops | bytes accessed | tf_op | source)
XLA Modules:
  0.0 186.8 jit_solution(409798083042916813)
XLA Ops:
  7.2 0.0 all-gather.9.cloned.1.call-start
  7.2 1.0 copy.21
  8.3 1.0 multiply_reduce_fusion.1
  9.3 0.7 compare_and_fusion
  10.0 0.9 convert_element_type.18
  10.9 0.8 gather_fusion
  11.7 1.1 multiply_reduce_fusion
  12.8 6.4 %all-gather = bf16[256,256]{1,0:T(8,128)(2,1)S(1)} all-gather(bf16[128,256]{1,0:T(8,128)(2,1)S(1)} %get-tuple-element.61), channel_id=2, replica_groups=mesh['blk_0'=2,'blk_1'=4,'blk_2'=8,'grp'=4] {'blk_0'}, dimensions={0}, use_global_device_ids=true | all-gather | bytes 196608 | tf_op jit(solution)/shard_map/all_gather | solution.py:22
  19.3 14.2 %all_gather.28 = bf16[8,128,256]{2,1,0:T(8,128)(2,1)} all-gather(bf16[2,128,256]{2,1,0:T(8,128)(2,1)S(1)} %bitcast.144), channel_id=1, replica_groups=mesh['blk_0'=2,'blk_1'=4,'blk_2'=8,'grp'=4] {'blk_1'}, dimensions={0}, use_global_device_ids=true | all-gather | bytes 655360 | tf_op jit(solution)/shard_map/all_gather | solution.py:22
  33.4 0.0 all-gather.9.cloned.1.call-update
  33.5 1.1 broadcast_in_dim.31
  34.6 5.6 %all-to-all-start = ((bf16[4,512,256]{2,1,0:T(8,128)(2,1)}), bf16[4,512,256]{2,1,0:T(8,128)(2,1)S(1)}, u32[]{:S(2)}, u32[]{:S(2)}) async-start(bf16[4,512,256]{2,1,0:T(8,128)(2,1)} %broadcast_in_dim.31), calls=%async_computation | async-start | bytes 2097152 | tf_op jit(solution)/shard_map/all_to_all | solution.py:35
  40.2 0.1 collective-permute-start
  41.0 13.4 %collective-permute-done = f32[128,256]{1,0:T(8,128)S(1)} collective-permute-done((f32[128,256]{1,0:T(8,128)}, f32[128,256]{1,0:T(8,128)S(1)}, u32[]{:S(2)}, u32[]{:S(2)}) %collective-permute-start) | collective-permute-done | bytes 131104 | tf_op jit(solution)/shard_map/ppermute | solution.py:72
  54.4 0.0 copy-start
  54.4 36.3 %all-gather.9.cloned.1.call-done = bf16[64,128,256]{2,1,0:T(8,128)(2,1)} async-done(((bf16[8,128,256]{2,1,0:T(8,128)(2,1)}), bf16[64,128,256]{2,1,0:T(8,128)(2,1)}) %all-gather.9.cloned.1.call-update) | async-done | bytes 4194320 | tf_op jit(solution)/shard_map/all_gather | solution.py:22
  90.7 4.6 %copy.8 = bf16[2,4,8,128,256]{4,3,2,1,0:T(8,128)(2,1)} copy(bf16[2,4,8,128,256]{4,3,0,1,2:T(8,128)(2,1)} %bitcast.140) | data formatting | bytes 8388608 | tf_op jit(solution)/shard_map/transpose | solution.py:26
  95.3 0.0 all-to-all-done
  95.3 0.0 copy-done
  95.3 38.3 %while.13 = (s32[]{:T(128)}, f32[8192]{0:T(1024)S(1)}, f32[8192]{0:T(1024)S(1)}, bf16[8,256,256]{2,1,0:T(8,128)(2,1)S(1)}, bf16[8192,256]{1,0:T(8,128)(2,1)}, /*index=5*/s32[]{:T(128)}, s32[]{:T(128)}) while((s32[]{:T(128)}, f32[8192]{0:T(1024)S(1)}, f32[8192]{0:T(1024)S(1)}, bf16[8,256,256]{2,1,0:T(8,128)(2,1)S(1)}, ...), condition=%wide.region_4.5_spmd.clone, body=%wide.region_1.4_spmd.clone.sunk | while | flops 1082171392 | bytes 21528676 | solution.py:100
  95.3 3.5 %fusion.40 = (f32[8192]{0:T(1024)S(1)}, f32[256,8192]{1,0:T(8,128)S(1)}) fusion(bf16[8192,256]{1,0:T(8,128)(2,1)} %get-tuple-element.149, bf16[8,256,256]{2,1,0:T(8,128)(2,1)S(1)} %get-tuple-element.148, s32[]{:T(128)S(6)} %copy.12), kind=kOutput, calls=%fused_computation.71.clone.1 | convolution fusion | flops 1077927936 | bytes 12746756 | tf_op jit(solution)/shard_map/while/body/eval_jaxpr/dot_general | solution.py:93
  98.9 1.2 exponential_reduce_fusion.2
  100.1 3.5 %fusion.40 = (f32[8192]{0:T(1024)S(1)}, f32[256,8192]{1,0:T(8,128)S(1)}) fusion(bf16[8192,256]{1,0:T(8,128)(2,1)} %get-tuple-element.149, bf16[8,256,256]{2,1,0:T(8,128)(2,1)S(1)} %get-tuple-element.148, s32[]{:T(128)S(6)} %copy.12), kind=kOutput, calls=%fused_computation.71.clone.1 | convolution fusion | flops 1077927936 | bytes 12746756 | tf_op jit(solution)/shard_map/while/body/eval_jaxpr/dot_general | solution.py:93
  103.6 1.2 exponential_reduce_fusion.2
  104.9 3.5 %fusion.40 = (f32[8192]{0:T(1024)S(1)}, f32[256,8192]{1,0:T(8,128)S(1)}) fusion(bf16[8192,256]{1,0:T(8,128)(2,1)} %get-tuple-element.149, bf16[8,256,256]{2,1,0:T(8,128)(2,1)S(1)} %get-tuple-element.148, s32[]{:T(128)S(6)} %copy.12), kind=kOutput, calls=%fused_computation.71.clone.1 | convolution fusion | flops 1077927936 | bytes 12746756 | tf_op jit(solution)/shard_map/while/body/eval_jaxpr/dot_general | solution.py:93
  108.4 1.2 exponential_reduce_fusion.2
  109.7 3.5 %fusion.40 = (f32[8192]{0:T(1024)S(1)}, f32[256,8192]{1,0:T(8,128)S(1)}) fusion(bf16[8192,256]{1,0:T(8,128)(2,1)} %get-tuple-element.149, bf16[8,256,256]{2,1,0:T(8,128)(2,1)S(1)} %get-tuple-element.148, s32[]{:T(128)S(6)} %copy.12), kind=kOutput, calls=%fused_computation.71.clone.1 | convolution fusion | flops 1077927936 | bytes 12746756 | tf_op jit(solution)/shard_map/while/body/eval_jaxpr/dot_general | solution.py:93
  113.2 1.2 exponential_reduce_fusion.2
  114.5 3.5 %fusion.40 = (f32[8192]{0:T(1024)S(1)}, f32[256,8192]{1,0:T(8,128)S(1)}) fusion(bf16[8192,256]{1,0:T(8,128)(2,1)} %get-tuple-element.149, bf16[8,256,256]{2,1,0:T(8,128)(2,1)S(1)} %get-tuple-element.148, s32[]{:T(128)S(6)} %copy.12), kind=kOutput, calls=%fused_computation.71.clone.1 | convolution fusion | flops 1077927936 | bytes 12746756 | tf_op jit(solution)/shard_map/while/body/eval_jaxpr/dot_general | solution.py:93
  118.0 1.2 exponential_reduce_fusion.2
  119.3 3.5 %fusion.40 = (f32[8192]{0:T(1024)S(1)}, f32[256,8192]{1,0:T(8,128)S(1)}) fusion(bf16[8192,256]{1,0:T(8,128)(2,1)} %get-tuple-element.149, bf16[8,256,256]{2,1,0:T(8,128)(2,1)S(1)} %get-tuple-element.148, s32[]{:T(128)S(6)} %copy.12), kind=kOutput, calls=%fused_computation.71.clone.1 | convolution fusion | flops 1077927936 | bytes 12746756 | tf_op jit(solution)/shard_map/while/body/eval_jaxpr/dot_general | solution.py:93
  122.8 1.2 exponential_reduce_fusion.2
  124.1 3.5 %fusion.40 = (f32[8192]{0:T(1024)S(1)}, f32[256,8192]{1,0:T(8,128)S(1)}) fusion(bf16[8192,256]{1,0:T(8,128)(2,1)} %get-tuple-element.149, bf16[8,256,256]{2,1,0:T(8,128)(2,1)S(1)} %get-tuple-element.148, s32[]{:T(128)S(6)} %copy.12), kind=kOutput, calls=%fused_computation.71.clone.1 | convolution fusion | flops 1077927936 | bytes 12746756 | tf_op jit(solution)/shard_map/while/body/eval_jaxpr/dot_general | solution.py:93
  127.6 1.2 exponential_reduce_fusion.2
  128.9 3.5 %fusion.40 = (f32[8192]{0:T(1024)S(1)}, f32[256,8192]{1,0:T(8,128)S(1)}) fusion(bf16[8192,256]{1,0:T(8,128)(2,1)} %get-tuple-element.149, bf16[8,256,256]{2,1,0:T(8,128)(2,1)S(1)} %get-tuple-element.148, s32[]{:T(128)S(6)} %copy.12), kind=kOutput, calls=%fused_computation.71.clone.1 | convolution fusion | flops 1077927936 | bytes 12746756 | tf_op jit(solution)/shard_map/while/body/eval_jaxpr/dot_general | solution.py:93
  132.4 1.2 exponential_reduce_fusion.2
  133.6 0.1 maximum_bitcast_fusion
  133.7 6.4 %all-gather.4 = f32[2,2,8192]{2,1,0:T(2,128)S(1)} all-gather(f32[1,2,8192]{2,1,0:T(2,128)S(1)} %maximum_bitcast_fusion), channel_id=3, replica_groups=mesh['blk_0'=2,'blk_1'=4,'blk_2'=8,'grp'=4] {'blk_0'}, dimensions={0}, use_global_device_ids=true | all-gather | bytes 196608 | tf_op jit(solution)/shard_map/all_gather | solution.py:51
  140.1 0.1 fusion.14
  140.3 0.1 maximum_bitcast_fusion.1
  140.3 12.7 %all-gather.5 = f32[4,2,8192]{2,1,0:T(2,128)S(1)} all-gather(f32[1,2,8192]{2,1,0:T(2,128)S(1)} %maximum_bitcast_fusion.1), channel_id=4, replica_groups=mesh['blk_0'=2,'blk_1'=4,'blk_2'=8,'grp'=4] {'blk_1'}, dimensions={0}, use_global_device_ids=true | all-gather | bytes 327680 | tf_op jit(solution)/shard_map/all_gather | solution.py:51
  153.1 0.3 fusion.5
  153.4 0.1 maximum_bitcast_fusion.2
  153.5 25.3 %all-gather.6 = f32[8,2,8192]{2,1,0:T(2,128)S(1)} all-gather(f32[1,2,8192]{2,1,0:T(2,128)S(1)} %maximum_bitcast_fusion.2), channel_id=5, replica_groups=mesh['blk_0'=2,'blk_1'=4,'blk_2'=8,'grp'=4] {'blk_2'}, dimensions={0}, use_global_device_ids=true | all-gather | bytes 589824 | tf_op jit(solution)/shard_map/all_gather | solution.py:51
  178.7 0.5 fusion.34
  179.3 0.1 multiply_add_fusion
  179.3 0.6 add_subtract_fusion
  (31 shorter events, 0.3 us)
Async XLA Ops:
  7.2 83.6 %all-gather.9.cloned.1.call-start = ((), (), s32[]{:S(2)}) async-start(), calls=%async_computation.1 | async-start | bytes 4718592 | tf_op jit(solution)/shard_map/all_gather | solution.py:22
  34.6 60.8 %all-to-all-start = ((bf16[4,512,256]{2,1,0:T(8,128)(2,1)}), bf16[4,512,256]{2,1,0:T(8,128)(2,1)S(1)}, u32[]{:S(2)}, u32[]{:S(2)}) async-start(bf16[4,512,256]{2,1,0:T(8,128)(2,1)} %broadcast_in_dim.31), calls=%async_computation | async-start | bytes 2097152 | tf_op jit(solution)/shard_map/all_to_all | solution.py:35
  40.2 14.2 %collective-permute-start = (f32[128,256]{1,0:T(8,128)}, f32[128,256]{1,0:T(8,128)S(1)}, u32[]{:S(2)}, u32[]{:S(2)}) collective-permute-start(f32[128,256]{1,0:T(8,128)} %param.9), channel_id=1, source_target_pairs={{0,1},{1,2},{2,3},{3,4},{4,5},{5,6},{6,7},{7,8},{8,9},{9,10},{10,1... | collective-permute-start | bytes 393224 | tf_op jit(solution)/shard_map/ppermute | solution.py:72
  54.4 40.9 %copy-start = (f32[512,256]{1,0:T(8,128)}, f32[512,256]{1,0:T(8,128)S(1)}, u32[]{:S(2)}) copy-start(f32[512,256]{1,0:T(8,128)S(1)} %constant_dynamic-update-slice_fusion) | copy-start | bytes 1572868
Sparse Core Ops, SparseCore 0:
  33.6 57.1 all-gather.8
where the time goes:
time: 187 us
  blocking collectives  65 us (35%)
  waiting for transfers between devices  49.7 us (27%)
  matrix products  27.9 us (15%)
  other arithmetic  15 us (8%)
  between operations  14.8 us (8%)
  local copies, waits for them, and re-layouts  8.14 us (4%)
  starting transfers between devices  5.78 us (3%)
    all_gather x3, blocking collectives, collected_together(): both, at, found = (lax.all_gather(jnp.concatenate(lines), axis), 0, {})  44.4 us
    all_gather x1, waiting for transfers between devices, gather_in_order(): pieces = lax.all_gather(pieces, axes[k], axis=0, tiled=True)  36.3 us
    dot_general x8, matrix products, one_block(): lax.dot_general(query_rows, key_block, (((1,), (1,)), ((), ())), preferre...  27.9 us
    all_gather x2, blocking collectives, gather_in_order(): pieces = lax.all_gather(pieces, axes[k], axis=0, tiled=True)  20.6 us
    ppermute x1, waiting for transfers between devices, from_behind(): return lax.ppermute(value, axis, pairs)  13.4 us
    reduce_sum x8, other arithmetic, one_block(): jnp.sum(jnp.exp(scores - new_top[:, None]), axis=1)  9.67 us
    all_to_all x1, starting transfers between devices, from_everyone(): lax.all_to_all(jnp.broadcast_to(x[None], (count, *x.shape)), axis, 0, 0,...  5.62 us
    transpose x1, local copies, waits for them, and re-layouts, gather_in_order(): pieces.transpose(*turned, *range(len(sequence), pieces.ndim))  4.62 us
  transfers between devices with their start and end apart: 3, of which 2 were waited for; matrix products, arithmetic and copies ran while one was open for 3% of the time, Pallas kernels for 0%

commit v1 on v0

--- a/solution.py
+++ b/solution.py
@@ -19,7 +19,10 @@
 def gather_in_order(x, axes, sequence):
     pieces = x[None]
     for k in sequence:
-        pieces = lax.all_gather(pieces, axes[k], axis=0, tiled=True)
+        n_dev = lax.axis_size(axes[k])
+        parts = jnp.stack([pieces for _ in range(n_dev)])
+        parts = lax.all_to_all(parts, axes[k], split_axis=0, concat_axis=0)
+        pieces = jnp.concatenate(parts, axis=0)
     block = [lax.axis_size(axes[k]) for k in reversed(sequence)]
     pieces = pieces.reshape(*block, *x.shape)
     turned = sorted(range(len(sequence)), key=lambda place: sequence[len(sequence) - 1 - place])

time: 187 us -> 242 us (1.29)
  waiting for transfers between devices: 49.7 us -> 107 us
  between operations: 14.8 us -> 1.41 us
  starting transfers between devices: 5.78 us -> 13.4 us
  local copies, waits for them, and re-layouts: 8.14 us -> 10.8 us
    all_to_all x0 -> x1, waiting for transfers between devices: none -> 93.5 us  [gather_in_order(): parts = lax.all_to_all(parts, axes[k], split_axis=0, concat_axis=0)]
    all_gather x1 -> x0, waiting for transfers between devices: 36.3 us -> none  [gather_in_order(): pieces = lax.all_gather(pieces, axes[k], axis=0, tiled=True)]
    all_to_all x0 -> x2, blocking collectives: none -> 21.5 us  [gather_in_order(): parts = lax.all_to_all(parts, axes[k], split_axis=0, concat_axis=0)]
    all_gather x2 -> x0, blocking collectives: 20.6 us -> none  [gather_in_order(): pieces = lax.all_gather(pieces, axes[k], axis=0, tiled=True)]
    all_to_all x0 -> x1, starting transfers between devices: none -> 8.47 us  [gather_in_order(): parts = lax.all_to_all(parts, axes[k], split_axis=0, concat_axis=0)]
    another operation x0 -> x2, local copies, waits for them, and re-layouts: none -> 2.5 us  [gather_in_order(): parts = jnp.stack([pieces for _ in range(n_dev)])]
  transfers between devices with their start and end apart: 3 -> 3, of which waited for: 2 -> 2; matrix products, arithmetic and copies ran while one was open for 3% -> 2% of each run, Pallas kernels for 0% -> 0%
where the time goes in v1:
time: 242 us
  waiting for transfers between devices  107 us (44%)
  blocking collectives  65.7 us (27%)
  matrix products  27.9 us (12%)
  other arithmetic  15 us (6%)
  starting transfers between devices  13.4 us (6%)
  local copies, waits for them, and re-layouts  10.8 us (4%)
    all_to_all x1, waiting for transfers between devices, gather_in_order(): parts = lax.all_to_all(parts, axes[k], split_axis=0, concat_axis=0)  93.5 us
    all_gather x3, blocking collectives, collected_together(): both, at, found = (lax.all_gather(jnp.concatenate(lines), axis), 0, {})  44.2 us
    dot_general x8, matrix products, one_block(): lax.dot_general(query_rows, key_block, (((1,), (1,)), ((), ())), preferre...  27.9 us
    all_to_all x2, blocking collectives, gather_in_order(): parts = lax.all_to_all(parts, axes[k], split_axis=0, concat_axis=0)  21.5 us
    ppermute x1, waiting for transfers between devices, from_behind(): return lax.ppermute(value, axis, pairs)  13.4 us
    reduce_sum x8, other arithmetic, one_block(): jnp.sum(jnp.exp(scores - new_top[:, None]), axis=1)  9.67 us
    all_to_all x1, starting transfers between devices, gather_in_order(): parts = lax.all_to_all(parts, axes[k], split_axis=0, concat_axis=0)  8.47 us
  transfers between devices with their start and end apart: 3, of which 2 were waited for; matrix products, arithmetic and copies ran while one was open for 2% of the time, Pallas kernels for 0%

profile of v1, /device:TPU:8, one launch (start us, length us, event | category | flops | bytes accessed | tf_op | source)
XLA Modules:
  0.0 241.6 jit_solution(14987305493462223286)
XLA Ops:
  0.6 1.0 copy.21
  1.7 1.0 multiply_reduce_fusion.1
  2.7 0.7 compare_and_fusion
  3.4 0.9 convert_element_type.18
  4.3 0.8 gather_fusion
  5.2 1.1 multiply_reduce_fusion
  6.3 9.3 %all_to_all.20 = bf16[2,1,128,256]{3,2,1,0:T(8,128)(2,1)S(1)} all-to-all(bf16[2,1,128,256]{3,2,1,0:T(8,128)(2,1)S(1)} %pad_maximum_fusion), channel_id=1, replica_groups=mesh['blk_0'=2,'blk_1'=4,'blk_2'=8,'grp'=4] {'blk_0'}, dimensions={0} | all-to-all | bytes 262144 | tf_op jit(solution)/shard_map/all_to_all | solution.py:24
  15.6 12.2 %all_to_all.21 = bf16[4,2,128,256]{3,2,1,0:T(8,128)(2,1)S(1)} all-to-all(bf16[4,2,128,256]{3,2,1,0:T(8,128)(2,1)S(1)} %stack.10), channel_id=1, replica_groups=mesh['blk_0'=2,'blk_1'=4,'blk_2'=8,'grp'=4] {'blk_1'}, dimensions={0} | all-to-all | bytes 1048576 | tf_op jit(solution)/shard_map/all_to_all | solution.py:24
  27.8 2.5 %stack.11 = bf16[8,8,128,256]{3,2,1,0:T(8,128)(2,1)} broadcast(bf16[8,128,256]{2,1,0:T(8,128)(2,1)S(1)} %bitcast.144), dimensions={1,2,3} | broadcast | bytes 4718592 | tf_op jit(solution)/shard_map/stack | solution.py:23
  30.3 8.5 %all-to-all-start.3 = ((bf16[8,8,128,256]{3,2,1,0:T(8,128)(2,1)}), bf16[8,8,128,256]{3,2,1,0:T(8,128)(2,1)}, u32[]{:S(2)}, u32[]{:S(2)}) async-start(bf16[8,8,128,256]{3,2,1,0:T(8,128)(2,1)} %stack.11), calls=%async_computation.3 | async-start | bytes 8388608 | tf_op jit(solution)/shard_map/all_to_all | solution.py:24
  38.8 93.5 %all-to-all-done.3 = bf16[8,8,128,256]{3,2,1,0:T(8,128)(2,1)} async-done(((bf16[8,8,128,256]{3,2,1,0:T(8,128)(2,1)}), bf16[8,8,128,256]{3,2,1,0:T(8,128)(2,1)}, u32[]{:S(2)}, u32[]{:S(2)}) %all-to-all-start.3) | async-done | bytes 4194336 | tf_op jit(solution)/shard_map/all_to_all | solution.py:24
  132.3 1.1 broadcast_in_dim.28
  133.4 4.8 %all-to-all-start = ((bf16[4,512,256]{2,1,0:T(8,128)(2,1)}), bf16[4,512,256]{2,1,0:T(8,128)(2,1)S(1)}, u32[]{:S(2)}, u32[]{:S(2)}) async-start(bf16[4,512,256]{2,1,0:T(8,128)(2,1)} %broadcast_in_dim.28), calls=%async_computation | async-start | bytes 2097152 | tf_op jit(solution)/shard_map/all_to_all | solution.py:38
  138.2 0.0 copy-done.1
  138.2 0.1 collective-permute-start
  139.0 13.4 %collective-permute-done = f32[128,256]{1,0:T(8,128)S(1)} collective-permute-done((f32[128,256]{1,0:T(8,128)S(1)}, f32[128,256]{1,0:T(8,128)S(1)}, u32[]{:S(2)}, u32[]{:S(2)}) %collective-permute-start) | collective-permute-done | bytes 131104 | tf_op jit(solution)/shard_map/ppermute | solution.py:75
  152.4 0.0 copy-start
  152.4 4.8 %copy.8 = bf16[2,4,8,128,256]{4,3,2,1,0:T(8,128)(2,1)} copy(bf16[2,4,8,128,256]{4,3,0,1,2:T(8,128)(2,1)} %bitcast.5) | data formatting | bytes 8388608 | tf_op jit(solution)/shard_map/transpose | solution.py:29
  157.2 0.0 all-to-all-done
  157.2 0.0 copy-done
  157.2 38.3 %while.13 = (s32[]{:T(128)}, f32[8192]{0:T(1024)S(1)}, f32[8192]{0:T(1024)S(1)}, bf16[8,256,256]{2,1,0:T(8,128)(2,1)S(1)}, bf16[8192,256]{1,0:T(8,128)(2,1)}, /*index=5*/s32[]{:T(128)}, s32[]{:T(128)}) while((s32[]{:T(128)}, f32[8192]{0:T(1024)S(1)}, f32[8192]{0:T(1024)S(1)}, bf16[8,256,256]{2,1,0:T(8,128)(2,1)S(1)}, ...), condition=%wide.region_4.5_spmd.clone, body=%wide.region_1.4_spmd.clone.sunk | while | flops 1082171392 | bytes 21528676 | solution.py:103
  157.2 3.5 %fusion.40 = (f32[8192]{0:T(1024)S(1)}, f32[256,8192]{1,0:T(8,128)S(1)}) fusion(bf16[8192,256]{1,0:T(8,128)(2,1)} %get-tuple-element.149, bf16[8,256,256]{2,1,0:T(8,128)(2,1)S(1)} %get-tuple-element.148, s32[]{:T(128)S(6)} %copy.12), kind=kOutput, calls=%fused_computation.72.clone.1 | convolution fusion | flops 1077927936 | bytes 12746756 | tf_op jit(solution)/shard_map/while/body/eval_jaxpr/dot_general | solution.py:96
  160.8 1.2 exponential_reduce_fusion.2
  162.0 3.5 %fusion.40 = (f32[8192]{0:T(1024)S(1)}, f32[256,8192]{1,0:T(8,128)S(1)}) fusion(bf16[8192,256]{1,0:T(8,128)(2,1)} %get-tuple-element.149, bf16[8,256,256]{2,1,0:T(8,128)(2,1)S(1)} %get-tuple-element.148, s32[]{:T(128)S(6)} %copy.12), kind=kOutput, calls=%fused_computation.72.clone.1 | convolution fusion | flops 1077927936 | bytes 12746756 | tf_op jit(solution)/shard_map/while/body/eval_jaxpr/dot_general | solution.py:96
  165.6 1.2 exponential_reduce_fusion.2
  166.8 3.5 %fusion.40 = (f32[8192]{0:T(1024)S(1)}, f32[256,8192]{1,0:T(8,128)S(1)}) fusion(bf16[8192,256]{1,0:T(8,128)(2,1)} %get-tuple-element.149, bf16[8,256,256]{2,1,0:T(8,128)(2,1)S(1)} %get-tuple-element.148, s32[]{:T(128)S(6)} %copy.12), kind=kOutput, calls=%fused_computation.72.clone.1 | convolution fusion | flops 1077927936 | bytes 12746756 | tf_op jit(solution)/shard_map/while/body/eval_jaxpr/dot_general | solution.py:96
  170.3 1.2 exponential_reduce_fusion.2
  171.6 3.5 %fusion.40 = (f32[8192]{0:T(1024)S(1)}, f32[256,8192]{1,0:T(8,128)S(1)}) fusion(bf16[8192,256]{1,0:T(8,128)(2,1)} %get-tuple-element.149, bf16[8,256,256]{2,1,0:T(8,128)(2,1)S(1)} %get-tuple-element.148, s32[]{:T(128)S(6)} %copy.12), kind=kOutput, calls=%fused_computation.72.clone.1 | convolution fusion | flops 1077927936 | bytes 12746756 | tf_op jit(solution)/shard_map/while/body/eval_jaxpr/dot_general | solution.py:96
  175.1 1.2 exponential_reduce_fusion.2
  176.4 3.5 %fusion.40 = (f32[8192]{0:T(1024)S(1)}, f32[256,8192]{1,0:T(8,128)S(1)}) fusion(bf16[8192,256]{1,0:T(8,128)(2,1)} %get-tuple-element.149, bf16[8,256,256]{2,1,0:T(8,128)(2,1)S(1)} %get-tuple-element.148, s32[]{:T(128)S(6)} %copy.12), kind=kOutput, calls=%fused_computation.72.clone.1 | convolution fusion | flops 1077927936 | bytes 12746756 | tf_op jit(solution)/shard_map/while/body/eval_jaxpr/dot_general | solution.py:96
  179.9 1.2 exponential_reduce_fusion.2
  181.2 3.5 %fusion.40 = (f32[8192]{0:T(1024)S(1)}, f32[256,8192]{1,0:T(8,128)S(1)}) fusion(bf16[8192,256]{1,0:T(8,128)(2,1)} %get-tuple-element.149, bf16[8,256,256]{2,1,0:T(8,128)(2,1)S(1)} %get-tuple-element.148, s32[]{:T(128)S(6)} %copy.12), kind=kOutput, calls=%fused_computation.72.clone.1 | convolution fusion | flops 1077927936 | bytes 12746756 | tf_op jit(solution)/shard_map/while/body/eval_jaxpr/dot_general | solution.py:96
  184.7 1.2 exponential_reduce_fusion.2
  186.0 3.5 %fusion.40 = (f32[8192]{0:T(1024)S(1)}, f32[256,8192]{1,0:T(8,128)S(1)}) fusion(bf16[8192,256]{1,0:T(8,128)(2,1)} %get-tuple-element.149, bf16[8,256,256]{2,1,0:T(8,128)(2,1)S(1)} %get-tuple-element.148, s32[]{:T(128)S(6)} %copy.12), kind=kOutput, calls=%fused_computation.72.clone.1 | convolution fusion | flops 1077927936 | bytes 12746756 | tf_op jit(solution)/shard_map/while/body/eval_jaxpr/dot_general | solution.py:96
  189.5 1.2 exponential_reduce_fusion.2
  190.8 3.5 %fusion.40 = (f32[8192]{0:T(1024)S(1)}, f32[256,8192]{1,0:T(8,128)S(1)}) fusion(bf16[8192,256]{1,0:T(8,128)(2,1)} %get-tuple-element.149, bf16[8,256,256]{2,1,0:T(8,128)(2,1)S(1)} %get-tuple-element.148, s32[]{:T(128)S(6)} %copy.12), kind=kOutput, calls=%fused_computation.72.clone.1 | convolution fusion | flops 1077927936 | bytes 12746756 | tf_op jit(solution)/shard_map/while/body/eval_jaxpr/dot_general | solution.py:96
  194.3 1.2 exponential_reduce_fusion.2
  195.5 0.1 maximum_bitcast_fusion
  195.6 6.4 %all-gather.3 = f32[2,2,8192]{2,1,0:T(2,128)S(1)} all-gather(f32[1,2,8192]{2,1,0:T(2,128)S(1)} %maximum_bitcast_fusion), channel_id=2, replica_groups=mesh['blk_0'=2,'blk_1'=4,'blk_2'=8,'grp'=4] {'blk_0'}, dimensions={0}, use_global_device_ids=true | all-gather | bytes 196608 | tf_op jit(solution)/shard_map/all_gather | solution.py:54
  202.0 0.1 fusion.14
  202.2 0.1 maximum_bitcast_fusion.1
  202.2 12.3 %all-gather.4 = f32[4,2,8192]{2,1,0:T(2,128)S(1)} all-gather(f32[1,2,8192]{2,1,0:T(2,128)S(1)} %maximum_bitcast_fusion.1), channel_id=3, replica_groups=mesh['blk_0'=2,'blk_1'=4,'blk_2'=8,'grp'=4] {'blk_1'}, dimensions={0}, use_global_device_ids=true | all-gather | bytes 327680 | tf_op jit(solution)/shard_map/all_gather | solution.py:54
  214.5 0.3 fusion.5
  214.8 0.1 maximum_bitcast_fusion.2
  214.9 25.5 %all-gather.5 = f32[8,2,8192]{2,1,0:T(2,128)S(1)} all-gather(f32[1,2,8192]{2,1,0:T(2,128)S(1)} %maximum_bitcast_fusion.2), channel_id=4, replica_groups=mesh['blk_0'=2,'blk_1'=4,'blk_2'=8,'grp'=4] {'blk_2'}, dimensions={0}, use_global_device_ids=true | all-gather | bytes 589824 | tf_op jit(solution)/shard_map/all_gather | solution.py:54
  240.4 0.5 fusion.34
  240.9 0.1 multiply_add_fusion
  241.0 0.6 add_subtract_fusion
  (34 shorter events, 0.4 us)
Async XLA Ops:
  27.8 110.4 %copy-start.1 = (f32[128,256]{1,0:T(8,128)S(1)}, f32[128,256]{1,0:T(8,128)}, u32[]{:S(2)}) copy-start(f32[128,256]{1,0:T(8,128)} %param.9) | copy-start | bytes 393220
  30.3 102.0 %all-to-all-start.3 = ((bf16[8,8,128,256]{3,2,1,0:T(8,128)(2,1)}), bf16[8,8,128,256]{3,2,1,0:T(8,128)(2,1)}, u32[]{:S(2)}, u32[]{:S(2)}) async-start(bf16[8,8,128,256]{3,2,1,0:T(8,128)(2,1)} %stack.11), calls=%async_computation.3 | async-start | bytes 8388608 | tf_op jit(solution)/shard_map/all_to_all | solution.py:24
  133.4 23.9 %all-to-all-start = ((bf16[4,512,256]{2,1,0:T(8,128)(2,1)}), bf16[4,512,256]{2,1,0:T(8,128)(2,1)S(1)}, u32[]{:S(2)}, u32[]{:S(2)}) async-start(bf16[4,512,256]{2,1,0:T(8,128)(2,1)} %broadcast_in_dim.28), calls=%async_computation | async-start | bytes 2097152 | tf_op jit(solution)/shard_map/all_to_all | solution.py:38
  138.2 14.2 %collective-permute-start = (f32[128,256]{1,0:T(8,128)S(1)}, f32[128,256]{1,0:T(8,128)S(1)}, u32[]{:S(2)}, u32[]{:S(2)}) collective-permute-start(f32[128,256]{1,0:T(8,128)S(1)} %copy-done.1), channel_id=1, source_target_pairs={{0,1},{1,2},{2,3},{3,4},{4,5},{5,6},{6,7},{7,8},{8,9},{9,10},{10,1... | collective-permute-start | bytes 393224 | tf_op jit(solution)/shard_map/ppermute | solution.py:75
  152.4 4.8 %copy-start = (f32[512,256]{1,0:T(8,128)}, f32[512,256]{1,0:T(8,128)S(1)}, u32[]{:S(2)}) copy-start(f32[512,256]{1,0:T(8,128)S(1)} %constant_dynamic-update-slice_fusion) | copy-start | bytes 1572868
